TPU v7x, 32 devices: a whole 2x2x4 slice. The times are simulated.
32 devices in a mesh: ice: 4 (over x, core), ocn: 8 (over z, y).
Axes of the slice: x: 2, y: 2, z: 4, core: 2. Of those that a mesh axis runs over, the one named last changes fastest.
Arguments:
- ice_state: bfloat16 [5, 20, 32768], P(None, None, ('ice', 'ocn')), may hold values from -6 to 6
- ocean_state: bfloat16 [5, 20, 32768], P(None, None, ('ice', 'ocn')), may hold values from -5 to 5
- ice_rate: float32 [5, 20], replicated, may hold values from 0.2 to 2
- block_weights: bfloat16 [1024, 128, 128], P(('ice', 'ocn')), may hold values from -0.375 to 0.375
- block_route: int32 [1024, 1], P(('ice', 'ocn')), may hold values from 0 to 31; in each aligned block of 32 rows (0 to 31, 32 to 63, ...) at most 2 rows name the same one
- block_tiles: int32 [1024, 2], P(('ice', 'ocn')), may hold values from 0 to 7
- block_valid: int32 [1024], P(('ice', 'ocn')), may hold values from 16 to 128
- ice_mask: int32 [32768], P(('ice', 'ocn')), may hold values 0 or 1
Outputs:
- ice_final: bfloat16 [5, 20, 32768], P(None, None, ('ice', 'ocn'))
- ocean_flux: bfloat16 [5, 20, 32768], P(None, None, ('ice', 'ocn'))
Inputs may be any that keep to these rules, and one draw needn't show every extreme that they name: `block_route`: among the blocks of one device no destination appears more than 2 times.
All inputs are finite; a program needn't handle non-finite values. No bound on the sum of `ice_mask` on one device may be relied on, other than what follows from the above.
Results may differ from a plain program's by a relative error of at most 0.008.
Values may be sent and summed in bfloat16 or wider, within the bound.
A program may use at most 128 MiB of HBM per device.

v0:
```python
import functools

import jax
import jax.numpy as jnp
from jax import lax
from jax.experimental import pallas as pl
from jax.experimental.pallas import tpu as pltpu
from jax.sharding import PartitionSpec as P

CAP = 2
AXES = ("ice", "ocn")
LINE = 4
ROWS = 8


def spread(first, count):
    return sorted(range(first, count), key=lambda c: min(c, count - c))


def kernel(
    sizes, parts, blk_ref, tile_ref, names_ref,
    ice_in, ocean_ref, rate_ref, land_ref, w_ref,
    ice_ref, flux_out,
    names_in, names, psend, prec, zsend, zrec, frec, bsend, ret, contrib, total,
    ns_s, ns_r, nl,
    ps_s, ps_r, zs_s, zs_r, fs_s, fs_r, bs_s, bs_r,
):
    Z, Y, N, tiles = sizes
    chans, width = ice_in.shape[1:]
    per = N * CAP
    ice_id, ocn_id = lax.axis_index("ice"), lax.axis_index("ocn")
    z, y = ocn_id // Y, ocn_id % Y
    p = ice_id * Y + y

    def plane(j):
        q = (p + j) % N
        return {"ice": q // Y, "ocn": z * Y + q % Y}

    def line(c):
        return {"ice": ice_id, "ocn": ((z + c) % Z) * Y + y}

    barrier = pltpu.get_barrier_semaphore()
    for j in range(1, N):
        pl.semaphore_signal(barrier, inc=1, device_id=plane(j), device_id_type=pl.DeviceIdType.MESH)
    for c in range(1, Z):
        pl.semaphore_signal(barrier, inc=1, device_id=line(c), device_id_type=pl.DeviceIdType.MESH)
    pl.semaphore_wait(barrier, N - 1 + Z - 1)

    def remote(src, dst, s, r, dev):
        return pltpu.make_async_remote_copy(
            src_ref=src, dst_ref=dst, send_sem=s, recv_sem=r,
            device_id=dev, device_id_type=pl.DeviceIdType.MESH,
        )

    def pcopy(h, c, j):
        at = pl.ds((c * N + j) * CAP, CAP)
        return remote(psend[h].at[at], prec[h].at[at], ps_s.at[h, c, j], ps_r.at[h, c, j], plane(j))

    def bcopy(h, c, j):
        at = pl.ds((c * N + j) * CAP, CAP)
        return remote(bsend[h].at[at], ret[h].at[at], bs_s.at[h, c, j], bs_r.at[h, c, j], plane(N - j))

    def zcopy(h, c):
        return remote(zsend[h].at[c], zrec[h].at[c], zs_s.at[h, c], zs_r.at[h, c], line(c))

    def fcopy(h, c):
        return remote(frec[h][0], frec[h][c], fs_s.at[h, c], fs_r.at[h, c], line(c))

    def ncopy(j):
        return remote(names_ref.at[j], names_in.at[j], ns_s.at[j], ns_r.at[j], plane(j))

    def nlocal(j):
        held = names_in if j else names_ref
        return pltpu.make_async_copy(held.at[j], names.at[j], nl.at[j])

    def name(c, n):
        return names[n // CAP, 0, c * CAP + n % CAP]

    for j in range(1, N):
        ncopy(j).start()
    nlocal(0).start()

    def here(h, at):
        return pl.ds(pl.multiple_of(parts[h][0] + at.start, ROWS), ROWS)

    def gather(h, load, place, start, finish):
        def rows(r, carry):
            at = pl.ds(pl.multiple_of(r * ROWS, ROWS), ROWS)

            def add(k, accs):
                x = load(k, at)
                to = jnp.full((ROWS, width), place(k), jnp.int32)
                return tuple(accs[t] + jnp.where(to == t, x, 0.0) for t in range(tiles))

            accs = lax.fori_loop(0, per, add, tuple(start(t, at) for t in range(tiles)), unroll=True)
            for t in range(tiles):
                finish(t, at, accs[t])
            return carry

        lax.fori_loop(0, parts[h][1] // ROWS, rows, 0)

    ice_ref[...] = ice_in[...]
    near = spread(1, Z)
    for j in range(1, N):
        ncopy(j).wait_recv()
        nlocal(j).start()
    for j in range(N):
        nlocal(j).wait()

    def forward(h):
        first, count = parts[h]
        for c in near[::-1] + [0]:
            for n in range(per):
                slot = c * per + n
                prod = jnp.dot(
                    ice_ref[tile_ref[slot] % tiles, pl.ds(first, count), :],
                    w_ref[blk_ref[slot]],
                    preferred_element_type=jnp.float32,
                ).astype(jnp.bfloat16)
                if n < CAP:
                    prec[h][slot] = prod
                else:
                    psend[h][slot] = prod
            for j in range(1, N):
                pcopy(h, c, j).start()

    def relay(h):
        for c in near[::-1] + [0]:
            for j in range(1, N):
                pcopy(h, c, j).wait_recv()
            base = c * per

            def load(k, at):
                return prec[h][base + k, at, :].astype(jnp.float32)

            def start(t, at):
                return jnp.zeros((ROWS, width), jnp.float32)

            def finish(t, at, acc):
                if c == 0:
                    total[t, here(h, at), :] = acc
                else:
                    zsend[h][c, t, at, :] = acc.astype(jnp.bfloat16)

            gather(h, load, lambda k: name(c, k), start, finish)
            if c:
                zcopy(h, c).start()

    def fluxes(h):
        for c in near:
            zcopy(h, c).wait_recv()

        def flux_rows(r, carry):
            at = pl.ds(pl.multiple_of(r * ROWS, ROWS), ROWS)
            for t in range(tiles):
                acc = total[t, here(h, at), :]
                for c in near:
                    acc = acc + zrec[h][c, t, at, :].astype(jnp.float32)
                acc = jnp.tanh(acc + ocean_ref[t, here(h, at), :].astype(jnp.float32))
                frec[h][0][t, at, :] = acc.astype(jnp.bfloat16)
                total[t, here(h, at), :] = jnp.zeros((ROWS, width), jnp.float32)
            return carry

        lax.fori_loop(0, parts[h][1] // ROWS, flux_rows, 0)
        for c in near:
            fcopy(h, c).start()
        picks(h, 0)

    def picks(h, c):
        held = (Z - c) % Z
        if c:
            fcopy(h, held).wait_recv()
        for n in range(per):
            slot = c * per + n
            tile = frec[h][held][name(c, n) % tiles]
            if n < CAP:
                ret[h][slot] = tile
            else:
                bsend[h][slot] = tile
        for j in range(1, N):
            bcopy(h, c, j).start()

    def replies(h):
        for c in near:
            picks(h, c)

    def finals(h):
        for c in [0] + near:
            for j in range(1, N):
                bcopy(h, c, j).wait_recv()
            base = c * per
            for n in range(per):
                contrib[n, : parts[h][1], :] = lax.dot_general(
                    ret[h][base + n], w_ref[blk_ref[base + n]], (((1,), (1,)), ((), ())),
                    preferred_element_type=jnp.float32,
                )

            def load(k, at):
                return contrib[k, at, :]

            def start(t, at):
                return total[t, here(h, at), :]

            def finish(t, at, acc):
                total[t, here(h, at), :] = acc

            gather(h, load, lambda k: tile_ref[base + k], start, finish)

        def ice_rows(r, carry):
            at = here(h, pl.ds(pl.multiple_of(r * ROWS, ROWS), ROWS))
            rate = rate_ref[at, :]
            for t in range(tiles):
                old = ice_ref[t, at, :].astype(jnp.float32)
                new = land_ref[pl.ds(t, 1), :] * (old + rate * jnp.tanh(total[t, at, :]))
                ice_ref[t, at, :] = new.astype(jnp.bfloat16)
            return carry

        lax.fori_loop(0, parts[h][1] // ROWS, ice_rows, 0)
        for c in range(Z):
            for j in range(1, N):
                pcopy(h, c, j).wait_send()
                bcopy(h, c, j).wait_send()
        for c in near:
            zcopy(h, c).wait_send()
            fcopy(h, c).wait_send()

    def turn(number, carry):
        relay(0)
        fluxes(0)
        relay(1)
        replies(0)
        fluxes(1)
        for h in range(2):
            finals(h)

            @pl.when(number == 0)
            def _():
                forward(h)

            if h == 0:
                replies(1)
        return carry

    forward(0)
    forward(1)
    lax.fori_loop(0, 2, turn, 0)
    for h in range(2):
        flux_out[:, pl.ds(parts[h][0], parts[h][1]), :] = frec[h][0][...]
    for j in range(1, N):
        ncopy(j).wait_send()


def on_device(
    ice_state, ocean_state, ice_rate, block_weights, block_route, block_tiles, block_valid, ice_mask
):
    cats, fields, cells = ice_state.shape
    chans = cats * fields
    rows = -(-chans // ROWS) * ROWS
    blocks, width, unused = block_weights.shape
    tiles = cells // width
    outer = lax.axis_size("ocn")
    Z = LINE if outer % LINE == 0 else outer
    Y = outer // Z
    N = lax.axis_size("ice") * Y
    ice_id, ocn_id = lax.axis_index("ice"), lax.axis_index("ocn")
    z, y = ocn_id // Y, ocn_id % Y
    p = ice_id * Y + y

    def number(q, zz):
        return ((q // Y) * outer + zz * Y + q % Y).astype(jnp.int32)

    route = block_route[:, 0]
    source, target = block_tiles[:, 0], block_tiles[:, 1]
    order = jnp.arange(blocks, dtype=jnp.int32)
    earlier = (route[None, :] == route[:, None]) & (order[None, :] < order[:, None])
    slot = jnp.sum(earlier.astype(jnp.int32), axis=1)
    js = jnp.arange(N, dtype=jnp.int32)
    cs = jnp.arange(Z, dtype=jnp.int32)
    ks = jnp.arange(CAP, dtype=jnp.int32)
    dest = number((p + js)[None, :] % N, ((z + cs) % Z)[:, None])
    code = route * CAP + slot
    sel = code == (dest[:, :, None] * CAP + ks)[..., None]
    blk = jnp.sum(jnp.where(sel, order, 0), axis=-1).reshape(-1)
    src = tiles + jnp.sum(jnp.where(sel, source - tiles, 0), axis=-1).reshape(-1)
    names = tiles + jnp.sum(jnp.where(sel, target - tiles, 0), axis=-1)
    names = names.transpose(1, 0, 2).reshape(N, 1, Z * CAP)
    names = jnp.pad(names, ((0, 0), (0, 0), (0, width - Z * CAP)))
    live = jnp.arange(width, dtype=jnp.int32)[None, :] < block_valid[:, None]
    masked = jnp.where(live[:, :, None], block_weights, jnp.zeros((), jnp.bfloat16))

    def tiled(values):
        values = values.reshape(chans, tiles, width).transpose(1, 0, 2)
        return jnp.pad(values, ((0, 0), (0, rows - chans), (0, 0)))

    ice = tiled(ice_state * ice_mask.astype(jnp.bfloat16)[None, None, :])
    ocean = tiled(ocean_state)
    rates = jnp.broadcast_to(jnp.pad(ice_rate.reshape(chans, 1), ((0, rows - chans), (0, 0))), (rows, width))
    land = ice_mask.astype(jnp.float32).reshape(tiles, width)
    slots = Z * N * CAP
    smem, vmem = pl.BlockSpec(memory_space=pltpu.SMEM), pl.BlockSpec(memory_space=pltpu.VMEM)
    tile = (rows, width)
    cut = rows // (2 * ROWS) * ROWS
    parts = ((0, cut), (cut, rows - cut))

    def both(*lead):
        return tuple(pltpu.VMEM(lead + (part[1], width), jnp.bfloat16) for part in parts)

    ice, flux = pl.pallas_call(
        functools.partial(kernel, (Z, Y, N, tiles), parts),
        out_shape=(jax.ShapeDtypeStruct((tiles,) + tile, jnp.bfloat16),) * 2,
        in_specs=[smem] * 2 + [vmem] * 6,
        out_specs=(vmem, vmem),
        scratch_shapes=[
            pltpu.VMEM((N, 1, width), jnp.int32),
            pltpu.SMEM((N, 1, width), jnp.int32),
            both(slots),
            both(slots),
            both(Z, tiles),
            both(Z, tiles),
            tuple(
                tuple(pltpu.VMEM((tiles, part[1], width), jnp.bfloat16) for c in range(Z))
                for part in parts
            ),
            both(slots),
            both(slots),
            pltpu.VMEM((N * CAP, rows - cut, width), jnp.float32),
            pltpu.VMEM((tiles,) + tile, jnp.float32),
            pltpu.SemaphoreType.DMA((N,)),
            pltpu.SemaphoreType.DMA((N,)),
            pltpu.SemaphoreType.DMA((N,)),
            pltpu.SemaphoreType.DMA((2, Z, N)),
            pltpu.SemaphoreType.DMA((2, Z, N)),
            pltpu.SemaphoreType.DMA((2, Z)),
            pltpu.SemaphoreType.DMA((2, Z)),
            pltpu.SemaphoreType.DMA((2, Z)),
            pltpu.SemaphoreType.DMA((2, Z)),
            pltpu.SemaphoreType.DMA((2, Z, N)),
            pltpu.SemaphoreType.DMA((2, Z, N)),
        ],
        compiler_params=pltpu.CompilerParams(
            collective_id=0, has_side_effects=True, vmem_limit_bytes=60 * 1024 * 1024
        ),
    )(blk, src, names, ice, ocean, rates, land, masked)

    def flat(values):
        return values[:, :chans].transpose(1, 0, 2).reshape(cats, fields, cells)

    return flat(ice), flat(flux)


def solution(mesh):
    placed = (
        P(None, None, ("ice", "ocn")),
        P(None, None, ("ice", "ocn")),
        P(),
        P(("ice", "ocn"), None, None),
        P(("ice", "ocn"), None),
        P(("ice", "ocn"), None),
        P(("ice", "ocn")),
        P(("ice", "ocn")),
    )
    return jax.shard_map(
        on_device,
        mesh=mesh,
        in_specs=placed,
        out_specs=(P(None, None, ("ice", "ocn")), P(None, None, ("ice", "ocn"))),
        check_vma=False,
    )
```

profile of v0, /device:TPU:0, one launch (start us, length us, event | category | flops | bytes accessed | tf_op | source)
XLA Modules:
  0.0 135.3 jit_solution(5862254812414421032)
XLA Ops:
  0.7 0.8 reshape.207
  1.5 0.9 convert_reduce_fusion
  2.4 0.7 multiply_add_fusion
  3.2 0.8 add_bitcast_fusion.1
  4.0 0.7 iota_compare_fusion
  4.7 1.4 %convert_bitcast_fusion = (f32[8,128]{1,0:T(8,128)}, bf16[1024]{0:T(1024)(128)(2,1)S(1)}) fusion(s32[1024]{0:T(1024)} %param.15), kind=kLoop, calls=%fused_computation.16 | loop fusion | flops 2048 | bytes 10240 | tf_op jit(solution)/shard_map/reshape | solution.py:298
  6.0 0.6 fusion.2
  6.7 0.6 pad.15.names_ref
  7.3 0.1 copy.19
  7.4 0.7 add.171.tile_ref
  8.1 0.1 copy.18
  8.2 0.6 reshape.203.blk_ref
  8.8 0.7 broadcast_in_dim.52.rate_ref
  9.5 0.1 reshape.206
  9.7 0.7 pad.17.ocean_ref
  10.4 0.3 copy-done.2
  10.8 0.1 reshape.205
  10.9 0.7 pad.16.ice_in
  11.6 1.5 %broadcast_select_fusion.w_ref = bf16[32,128,128]{2,1,0:T(8,128)(2,1)} fusion(bf16[32,128,128]{2,1,0:T(8,128)(2,1)S(1)} %copy-done, pred[32,128]{1,0:T(8,128)(4,1)S(1)} %iota_compare_fusion), kind=kLoop, calls=%fused_computation | loop fusion | flops 524288 | bytes 2101248 | tf_op jit(solution)/shard_map/jit(_where)/select_n | solution.py:289
  13.1 119.3 %shard_map.95 = (bf16[8,104,128]{2,1,0:T(8,128)(2,1)}, bf16[8,104,128]{2,1,0:T(8,128)(2,1)}) custom-call(s32[64]{0:T(128)} %reshape.203.blk_ref, s32[64]{0:T(128)} %add.171.tile_ref, s32[8,1,128]{2,1,0:T(1,128)} %pad.15.names_ref, bf16[8,104,128]{2,1,0:T(8,128)(2,1)} %pad.16.ice_in, bf16[8,104,128]{2,1,0:T(8,128)(2,1)} %pad.17.ocean_ref, ...), custom_call_target="tpu_custom_call" | custom-call | tf_op jit(solution)/shard_map/pallas_call | solution.py:308
  132.5 0.9 slice_bitcast_fusion.1
  133.5 0.8 reshape.209
  134.3 0.1 copy-done.3
  134.5 0.8 reshape.210
  (20 shorter events, 0.4 us)
Async XLA Ops:
  0.6 8.9 %copy-start.1 = (bf16[5,20,1024]{2,1,0:T(8,128)(2,1)S(1)}, bf16[5,20,1024]{2,1,0:T(8,128)(2,1)}, u32[]{:S(2)}) copy-start(bf16[5,20,1024]{2,1,0:T(8,128)(2,1)} %param.9) | copy-start | bytes 614404
  9.7 1.0 copy-start.2
  9.7 1.9 %copy-start = (bf16[32,128,128]{2,1,0:T(8,128)(2,1)S(1)}, bf16[32,128,128]{2,1,0:T(8,128)(2,1)}, u32[]{:S(2)}) copy-start(bf16[32,128,128]{2,1,0:T(8,128)(2,1)} %param.11) | copy-start | bytes 3145732
  133.5 0.9 copy-start.3
where the time goes:
time: 136 us; the launch traced here: 135 us
  Pallas kernels  119 us (88%)
  local copies, waits for them, and re-layouts  8.57 us (6%)
  other arithmetic  6.63 us (5%)
    pallas_call x1, Pallas kernels, on_device(): pl.pallas_call(functools.partial(kernel, (Z, Y, N, tiles), parts), out_sh...  119 us

commit v1 on v0

v1 whole, which is shorter than its diff:
```python
import functools

import jax
import jax.numpy as jnp
from jax import lax
from jax.experimental import pallas as pl
from jax.experimental.pallas import tpu as pltpu
from jax.sharding import PartitionSpec as P

CAP = 2
CORES = 2
LINE = 4
LANES = 128
AXES = ("ice", "ocn")
SPAN = 256


def order(count, calls):
    steps = []
    for h in range(count):
        for place, call in zip((0, 1, 5, 7, 12, 16, 22), calls):
            steps.append((3 * h + place, h, call))
    return [step[1:] for step in sorted(steps, key=lambda step: step[:2])]


def kernel(
    sizes, parts,
    route_ref, tiles_ref, valid_ref, rate_ref, land_hbm, ice_hbm, ocean_hbm, w_hbm,
    ice_out, flux_out,
    w_in, wsend, wall, tabv, tabs, namv, nams, rates, res, fres, sea, psend, prec,
    ice_g, fb, own, dsend, drec, zsend, zrec, zrel, csend, crec, mine,
    wl, tl, nl, ns_s, ns_r, ws_s, ws_r, ps_s, ps_r, as_s, as_r, ds_s, ds_r, zs_s, zs_r, rl_s, rl_r,
    fs_s, fs_r, fr_s, gs_s, gs_r, cs_s, cs_r, land_ref, ice_in, ocean_in, il,
):
    X, Y, Z, tiles, blocks = sizes
    Q = X * Y
    H = len(parts)
    per = CORES * CAP
    slots = Z * per
    outer = Z * Y
    cats, fields = rate_ref.shape
    ice_id, ocn_id = lax.axis_index("ice"), lax.axis_index("ocn")
    x, c = ice_id // CORES, ice_id % CORES
    z, y = ocn_id // Y, ocn_id % Y
    side = z // (Z // 2)
    zord = ((Z - 1) * (1 - side), Z // 2 - side, z + 1 - 2 * (z % 2), z)
    is_end = z == (Z - 1) * side
    is_mid = z != (Z - 1) * side

    def chip(j, back=False):
        dx, dy = j // Y, j % Y
        if back:
            dx, dy = X - dx, Y - dy
        return {"ice": ((x + dx) % X) * CORES + c, "ocn": z * Y + (y + dy) % Y}

    partner = {"ice": x * CORES + 1 - c, "ocn": ocn_id}

    def line(zt):
        return {"ice": ice_id, "ocn": zt * Y + y}

    def remote(src, dst, s, r, dev):
        return pltpu.make_async_remote_copy(
            src_ref=src, dst_ref=dst, send_sem=s, recv_sem=r,
            device_id=dev, device_id_type=pl.DeviceIdType.MESH,
        )

    wload = pltpu.make_async_copy(w_hbm, w_in, wl)
    loads = [
        pltpu.make_async_copy(src, dst, il.at[i])
        for i, (src, dst) in enumerate(((land_hbm, land_ref), (ice_hbm, ice_in), (ocean_hbm, ocean_in)))
    ]
    for load in loads:
        load.start()
    wload.start()

    hops = {j: min(j // Y, X - j // Y) + min(j % Y, Y - j % Y) for j in range(Q)}
    near = sorted(range(1, Q), key=hops.get)

    barrier = pltpu.get_barrier_semaphore()
    for j in range(1, Q):
        pl.semaphore_signal(barrier, inc=1, device_id=chip(j), device_id_type=pl.DeviceIdType.MESH)
    for i in range(1, Z):
        pl.semaphore_signal(barrier, inc=1, device_id=line((z + i) % Z), device_id_type=pl.DeviceIdType.MESH)
    pl.semaphore_signal(barrier, inc=1, device_id=partner, device_id_type=pl.DeviceIdType.MESH)

    def acopy(h, j):
        return remote(ice_g[h].at[0], ice_g[h].at[j], as_s.at[h, j], as_r.at[h, j], chip(j))

    def ncopy(j):
        return remote(namv.at[j], namv.at[Q + j], ns_s.at[j], ns_r.at[j], chip(j))

    def wcopy(j):
        return remote(wsend.at[j], wall.at[j], ws_s.at[j], ws_r.at[j], chip(j))

    def pcopy(h, g, j):
        at = pl.ds(zord[g] * per, per)
        return remote(psend[h].at[j, at], prec[h].at[j, at], ps_s.at[h, g, j], ps_r.at[h, g, j], chip(j))

    def dcopy(h, zd):
        return remote(dsend[h].at[zd], drec[h].at[zd], ds_s.at[h, zd], ds_r.at[h, zd], partner)

    def zcopy(h, zd):
        return remote(zsend[h].at[zd], zrec[h].at[z], zs_s.at[h, zd], zs_r.at[h, z], line(zd))

    def zwait(h, zs):
        remote(zsend[h].at[zs], zrec[h].at[zs], zs_s.at[h, zs], zs_r.at[h, zs], line(zs)).wait_recv()

    def rcopy(h, g):
        return remote(zsend[h].at[zord[g]], zrel[h].at[g], rl_s.at[h, g], rl_r.at[h, g], line(zord[2]))

    def fcopy(h, zt):
        return remote(fb[h].at[c, z], fb[h].at[c, z], fs_s.at[h, zt], fs_r.at[h, z], line(zt))

    def fwait(h, zs):
        remote(fb[h].at[c, zs], fb[h].at[c, zs], fs_s.at[h, zs], fs_r.at[h, zs], line(zs)).wait_recv()

    def frelay(h, g):
        held = fb[h].at[c, zord[g]]
        return remote(held, held, fr_s.at[h, g], fs_r.at[h, zord[g]], line(zord[2]))

    def gcopy(h, zs):
        return remote(fb[h].at[c, zs], fb[h].at[c, zs], gs_s.at[h, zs], gs_r.at[h, zs], partner)

    def gwait(h, zs):
        held = fb[h].at[1 - c, zs]
        remote(held, held, gs_s.at[h, zs], gs_r.at[h, zs], partner).wait_recv()

    def ccopy(h, j):
        return remote(csend[h].at[j], crec[h].at[j], cs_s.at[h, j], cs_r.at[h, j], chip(j, True))

    def lanes(t):
        return pl.ds(t * LANES, LANES)

    def land(t):
        return land_ref[pl.ds(t, 1), :].astype(jnp.float32)

    tall = -(-Q // 8) * 8
    sub = lax.broadcasted_iota(jnp.int32, (tall, LANES), 0)
    lane = lax.broadcasted_iota(jnp.int32, (tall, LANES), 1)
    base = jnp.zeros((tall, LANES), jnp.int32)
    for j in range(Q):
        dx, dy = j // Y, j % Y
        own_base = ((x + dx) % X) * CORES * outer + (y + dy) % Y
        base = jnp.where(sub == j, own_base, base)
    turn_of = lane & (CAP - 1)
    core_of = lax.shift_right_logical(lane, CAP.bit_length() - 1) & (CORES - 1)
    line_of = lax.shift_right_logical(lane, per.bit_length() - 1)
    dest = base + core_of * outer + line_of * Y

    def enter(b, carry):
        seen, code, name = carry
        hit = dest == route_ref[0, b]
        take = hit & (seen == turn_of)
        label = tiles_ref[0, b] * tiles + tiles_ref[1, b]
        code = jnp.where(take, (b * SPAN + valid_ref[b]) * (tiles * tiles) + label, code)
        name = jnp.where(take, label, name)
        return seen + jnp.where(hit, 1, 0), code, name

    none = jnp.zeros((tall, LANES), jnp.int32)
    unused, code, name = lax.fori_loop(0, blocks, enter, (none, none, none), unroll=8)
    for j in range(Q):
        tabv[j] = code[j : j + 1, :]
        namv[j] = name[j : j + 1, :]
    tload = pltpu.make_async_copy(tabv, tabs, tl)
    tload.start()

    for load in loads:
        load.wait()
    chans, padded = cats * fields, rates.shape[0]
    for t in range(tiles):
        if chans < padded:
            spare = jnp.zeros((8, LANES), jnp.float32)
            res[t, pl.ds(padded - 8, 8), :] = spare
            sea[t, pl.ds(padded - 8, 8), :] = spare
        for r in range(cats):
            at = pl.ds(r * fields, fields)
            res[t, at, :] = ice_in[r, :, lanes(t)].astype(jnp.float32) * land(t)
            sea[t, at, :] = ocean_in[r, :, lanes(t)].astype(jnp.float32)
    if chans < padded:
        rates[pl.ds(padded - 8, 8), :] = jnp.zeros((8, LANES), jnp.float32)
    for h, (first, count) in enumerate(parts):
        for t in range(tiles):
            ice_g[h][0, t] = res[t, pl.ds(first, count), :].astype(jnp.bfloat16)

    pl.semaphore_wait(barrier, Q - 1 + Z - 1 + 1)
    for j in range(1, Q):
        ncopy(j).start()
    nload = [
        pltpu.make_async_copy(namv.at[j if j == 0 else Q + j], nams.at[j], nl.at[j]) for j in range(Q)
    ]
    nload[0].start()
    tload.wait()
    wload.wait()

    rows = lax.broadcasted_iota(jnp.int32, (LANES, LANES), 0)

    def block(j, n):
        v = tabs[j, 0, n] // (tiles * tiles)
        held = w_in[v // SPAN]
        return jnp.where(rows < v % SPAN, held, jnp.zeros((), jnp.bfloat16))

    def products(h, j, n, held):
        v = tabs[j, 0, n] % (tiles * tiles)
        prod = jnp.dot(ice_g[h][0, v // tiles], held, preferred_element_type=jnp.float32)
        return prod.astype(jnp.bfloat16)

    for g in range(Z):
        def put(i, carry):
            j = Q - 1 - i
            for k in range(per):
                n = zord[g] * per + k
                held = block(j, n)
                wsend[j, n] = held
                for h in range(H):
                    psend[h][j, n] = products(h, j, n, held)
            for h in range(H):
                pcopy(h, g, j).start()
            return carry

        lax.fori_loop(0, Q - 1, put, 0)
    for j in near:
        wcopy(j).start()

    def keep(zd, carry):
        for k in range(per):
            n = zd * per + k
            held = block(0, n)
            wall[0, n] = held
            for h in range(H):
                prec[h][0, n] = products(h, 0, n, held)
        return carry

    lax.fori_loop(0, Z, keep, 0)
    for r in range(cats):
        for f in range(fields):
            rates[pl.ds(r * fields + f, 1), :] = jnp.full((1, LANES), rate_ref[r, f], jnp.float32)
    for j in range(1, Q):
        ncopy(j).wait_recv()
        nload[j].start()
    for j in range(Q):
        nload[j].wait()

    def spread(count, index, prod, accs):
        at = jnp.full((count, LANES), index, jnp.int32)
        return tuple(accs[t] + jnp.where(at == t, prod, 0.0) for t in range(tiles))

    def forward(h, zd, ready=False):
        count = parts[h][1]
        start = tuple(jnp.zeros((count, LANES), jnp.float32) for t in range(tiles))

        def sums(core):
            def add(j, accs):
                for k in range(CAP):
                    n = zd * per + core * CAP + k
                    v = nams[j, 0, n]
                    if ready:
                        prod = prec[h][j, n].astype(jnp.float32)
                    else:
                        prod = jnp.dot(ice_g[h][j, v // tiles], wall[j, n], preferred_element_type=jnp.float32)
                    accs = spread(count, v % tiles, prod, accs)
                return accs

            return lax.fori_loop(0, Q, add, start, unroll=min(Q, 4))

        accs = sums(1 - c)
        for t in range(tiles):
            dsend[h][zd, t] = accs[t].astype(jnp.bfloat16)
        dcopy(h, zd).start()
        accs = sums(c)
        for t in range(tiles):
            own[h][zd, t] = accs[t]

    def merge(h, g):
        zd = zord[g]
        dcopy(h, zd).wait_recv()

        def put():
            for t in range(tiles):
                zsend[h][zd, t] = (own[h][zd, t] + drec[h][zd, t].astype(jnp.float32)).astype(jnp.bfloat16)

        if g < 2:
            @pl.when(is_end)
            def _():
                put()
                rcopy(h, g).start()
        elif g == 2:
            put()
            zcopy(h, zd).start()

    def relay(h, which=(0, 1)):
        @pl.when(is_mid)
        def _():
            for g in which:
                zd = zord[g]
                rcopy(h, g).wait_recv()
                for t in range(tiles):
                    acc = own[h][zd, t] + drec[h][zd, t].astype(jnp.float32) + zrel[h][g, t].astype(jnp.float32)
                    zsend[h][zd, t] = acc.astype(jnp.bfloat16)
                zcopy(h, zd).start()

    def flux(h):
        first, count = parts[h]
        zwait(h, zord[2])
        zwait(h, zord[1])
        for t in range(tiles):
            acc = own[h][z, t] + drec[h][z, t].astype(jnp.float32)
            for g in (2, 1):
                acc = acc + zrec[h][zord[g], t].astype(jnp.float32)
            acc = jnp.tanh(acc + sea[t, pl.ds(first, count), :])
            fb[h][c, z, t] = acc.astype(jnp.bfloat16)
            fres[t, pl.ds(first, count), :] = acc

        fcopy(h, zord[1]).start()
        fcopy(h, zord[2]).start()
        gcopy(h, z).start()

    def arrivals(h):
        def take(g):
            fwait(h, zord[g])
            gcopy(h, zord[g]).start()

        @pl.when(is_mid)
        def _():
            for g in (1, 0):
                fwait(h, zord[g])
                frelay(h, g).start()
                gcopy(h, zord[g]).start()
            take(2)

        @pl.when(is_end)
        def _():
            for g in (2, 1, 0):
                take(g)

    def back(h, j):
        count = parts[h][1]
        accs = tuple(jnp.zeros((count, LANES), jnp.float32) for t in range(tiles))
        for n in range(slots):
            zd, core = n // per, n // CAP % CORES
            v = nams[j, 0, n]
            prod = lax.dot_general(
                fb[h][core, zd, v % tiles], wall[j, n], (((1,), (1,)), ((), ())),
                preferred_element_type=jnp.float32,
            )
            accs = spread(count, v // tiles, prod, accs)
        return accs

    def fluxes(h):
        for zs in range(Z):
            gwait(h, zs)

    def give(h, j):
        accs = back(h, j)
        for t in range(tiles):
            csend[h][j, t] = accs[t].astype(jnp.bfloat16)
        ccopy(h, j).start()

    def hold(h):
        accs = back(h, 0)
        for t in range(tiles):
            mine[h][t] = accs[t]

    def backward(h):
        fluxes(h)

        def one(i, carry):
            give(h, Q - 1 - i)
            return carry

        lax.fori_loop(0, Q - 1, one, 0)
        hold(h)

    def finish(h, number):
        first, count = parts[h]
        for j in range(Q - 1, 0, -1):
            ccopy(h, j).wait_recv()
        if number:
            for j in range(1, Q):
                acopy(h, j).wait_send()
        rate = rates[pl.ds(first, count), :]
        for t in range(tiles):
            acc = mine[h][t]
            for j in range(1, Q):
                acc = acc + crec[h][j, t].astype(jnp.float32)
            old = ice_g[h][0, t].astype(jnp.float32)
            new = land(t) * (old + rate * jnp.tanh(acc))
            if number:
                res[t, pl.ds(first, count), :] = new
            else:
                ice_g[h][0, t] = new.astype(jnp.bfloat16)
        if not number:
            for j in range(Q - 1, 0, -1):
                acopy(h, j).start()

        for j in range(1, Q):
            ccopy(h, j).wait_send()
        for zd in range(Z):
            dcopy(h, zd).wait_send()
            gcopy(h, zd).wait_send()
        zcopy(h, zord[2]).wait_send()
        for g in (1, 2):
            fcopy(h, zord[g]).wait_send()

        @pl.when(is_end)
        def _():
            for g in range(2):
                rcopy(h, g).wait_send()

        @pl.when(is_mid)
        def _():
            for g in range(2):
                zcopy(h, zord[g]).wait_send()
                frelay(h, g).wait_send()

    def arrive(h):
        for j in range(Q - 1, 0, -1):
            acopy(h, j).wait_recv()

    def again(h):
        arrive(h)

        def one(zd, carry):
            forward(h, zd)
            return carry

        lax.fori_loop(0, Z, one, 0)

    def merges(h):
        for g in range(Z):
            merge(h, g)

    for g in range(Z):
        for h in range(H):
            for j in range(Q - 1, 0, -1):
                pcopy(h, g, j).wait_recv()
            forward(h, zord[g], True)
        for h in range(H):
            merge(h, g)
        if 0 < g < 3:
            for h in range(H):
                relay(h, (g - 1,))
    for h in range(H):
        flux(h)

    def rest(h):
        def one(i, carry):
            give(h, Q - 1 - i)
            return carry

        fluxes(h)
        lax.fori_loop(0, Q - 1, one, 0)
        hold(h)

    last_near = len(near) - max(1, Q // 4)
    for h in range(2):
        arrivals(h)
    fluxes(0)
    for j in near[:last_near]:
        wcopy(j).wait_recv()
        give(0, j)
    for h in range(2, H):
        arrivals(h)
    for j in near[last_near:]:
        wcopy(j).wait_recv()
        give(0, j)
    hold(0)
    for h in range(1, H):
        rest(h)
        finish(h - 1, 0)
    again(0)
    merges(0)
    finish(H - 1, 0)
    for j in range(1, Q):
        wcopy(j).wait_send()
        ncopy(j).wait_send()
        for h in range(H):
            for g in range(Z):
                pcopy(h, g, j).wait_send()

    def send(r, held, out):
        for t in range(tiles):
            out[r, :, lanes(t)] = held[t, pl.ds(r * fields, fields), :].astype(jnp.bfloat16)

    def last(h):
        if h == H - 1:
            for r in range(cats):
                send(r, fres, flux_out)
        finish(h, 1)
        first, count = parts[h]
        for r in range(cats):
            if first < (r + 1) * fields <= first + count:
                send(r, res, ice_out)

    for h, call in order(H, (again, merges, relay, flux, arrivals, backward, last)):
        if h or call not in (again, merges):
            call(h)


def cut(chans):
    rows = -(-chans // 8) * 8
    sizes = [32] * (rows // 32 - 1)
    sizes.append(rows - sum(sizes))
    parts, first = [], 0
    for size in sizes:
        parts.append((first, size))
        first += size
    return tuple(parts)


def on_device(
    ice_state, ocean_state, ice_rate, block_weights, block_route, block_tiles, block_valid, ice_mask
):
    cats, fields, cells = ice_state.shape
    chans = cats * fields
    blocks, width, unused = block_weights.shape
    tiles = cells // width
    outer = lax.axis_size("ocn")
    Z = LINE
    Y = outer // Z
    X = lax.axis_size("ice") // CORES
    Q = X * Y
    slots = Z * CORES * CAP
    assert outer % LINE == 0
    parts = cut(chans)
    H = len(parts)
    rows = sum(part[1] for part in parts)

    def each(*lead, dtype=jnp.bfloat16):
        return tuple(pltpu.VMEM(lead + (part[1], width), dtype) for part in parts)

    def sems(*shape):
        return pltpu.SemaphoreType.DMA(shape)

    smem, vmem = pl.BlockSpec(memory_space=pltpu.SMEM), pl.BlockSpec(memory_space=pltpu.VMEM)
    ice, flux = pl.pallas_call(
        functools.partial(kernel, (X, Y, Z, tiles, blocks), parts),
        out_shape=(jax.ShapeDtypeStruct(ice_state.shape, jnp.bfloat16),) * 2,
        in_specs=[smem] * 4 + [pl.BlockSpec(memory_space=pltpu.HBM)] * 4,
        out_specs=(vmem, vmem),
        scratch_shapes=[
            pltpu.VMEM((blocks, width, width), jnp.bfloat16),
            pltpu.VMEM((Q, slots, width, width), jnp.bfloat16),
            pltpu.VMEM((Q, slots, width, width), jnp.bfloat16),
            pltpu.VMEM((Q, 1, width), jnp.int32),
            pltpu.SMEM((Q, 1, width), jnp.int32),
            pltpu.VMEM((2 * Q, 1, width), jnp.int32),
            pltpu.SMEM((Q, 1, width), jnp.int32),
            pltpu.VMEM((rows, width), jnp.float32),
            pltpu.VMEM((tiles, rows, width), jnp.float32),
            pltpu.VMEM((tiles, rows, width), jnp.float32),
            pltpu.VMEM((tiles, rows, width), jnp.float32),
            each(Q, slots),
            each(Q, slots),
            each(Q, tiles),
            each(CORES, Z, tiles),
            each(Z, tiles, dtype=jnp.float32),
            each(Z, tiles),
            each(Z, tiles),
            each(Z, tiles),
            each(Z, tiles),
            each(2, tiles),
            each(Q, tiles),
            each(Q, tiles),
            each(tiles, dtype=jnp.float32),
            pltpu.SemaphoreType.DMA,
            pltpu.SemaphoreType.DMA,
            sems(Q), sems(Q), sems(Q),
            sems(Q), sems(Q),
            sems(H, Z, Q), sems(H, Z, Q),
            sems(H, Q), sems(H, Q),
            sems(H, Z), sems(H, Z),
            sems(H, Z), sems(H, Z),
            sems(H, 2), sems(H, 2),
            sems(H, Z), sems(H, Z),
            sems(H, 2),
            sems(H, Z), sems(H, Z),
            sems(H, Q), sems(H, Q),
            pltpu.VMEM((tiles, width), jnp.int32),
            pltpu.VMEM(ice_state.shape, jnp.bfloat16),
            pltpu.VMEM(ice_state.shape, jnp.bfloat16),
            sems(3),
        ],
        compiler_params=pltpu.CompilerParams(
            collective_id=0, has_side_effects=True, vmem_limit_bytes=60 * 1024 * 1024
        ),
    )(
        block_route.T, block_tiles.T, block_valid, ice_rate, ice_mask.reshape(tiles, width),
        ice_state, ocean_state, block_weights,
    )
    return ice, flux


def solution(mesh):
    placed = (
        P(None, None, AXES), P(None, None, AXES), P(), P(AXES, None, None),
        P(AXES, None), P(AXES, None), P(AXES), P(AXES),
    )
    return jax.shard_map(
        on_device, mesh=mesh, in_specs=placed,
        out_specs=(P(None, None, AXES), P(None, None, AXES)), check_vma=False,
    )
```

time: 136 us -> 112 us (0.82)
  Pallas kernels: 119 us -> 109 us
  other arithmetic: 6.63 us -> 0 us
  local copies, waits for them, and re-layouts: 8.57 us -> 2.39 us
    pallas_call x1, Pallas kernels: 119 us -> 109 us  [on_device(): pl.pallas_call(functools.partial(kernel, (X, Y, Z, tiles, blocks), parts)...]
    reshape x9 -> x0, local copies, waits for them, and re-layouts: 3.53 us -> none  [the longest x2 1.65 us: flat(): return values[:, :chans].transpose(1, 0, 2).reshape(cats, fields, cells)]
    pad x3 -> x0, local copies, waits for them, and re-layouts: 2.01 us -> none  [the longest x2 1.41 us: tiled(): return jnp.pad(values, ((0, 0), (0, rows - chans), (0, 0)))]
    unnamed x8 -> x4, local copies, waits for them, and re-layouts: 0.41 us -> 2.39 us
    select_n x2 -> x0, other arithmetic: 1.52 us -> none  [the longest x1 1.5 us: on_device(): jnp.where(live[:, :, None], block_weights, jnp.zeros((), jnp.bfloat16))]
    reduce_sum x2 -> x0, other arithmetic: 1.48 us -> none  [the longest x1 0.91 us: on_device(): slot = jnp.sum(earlier.astype(jnp.int32), axis=1)]
where the time goes in v1:
time: 112 us
  Pallas kernels  109 us (97%)
  local copies, waits for them, and re-layouts  2.39 us (2%)
    pallas_call x1, Pallas kernels, on_device(): pl.pallas_call(functools.partial(kernel, (X, Y, Z, tiles, blocks), parts)...  109 us
    unnamed x4, local copies, waits for them, and re-layouts  2.39 us

profile of v1, /device:TPU:0, one launch (start us, length us, event | category | flops | bytes accessed | tf_op | source)
XLA Modules:
  0.0 112.0 jit_solution(11521914921283016864)
XLA Ops:
  0.6 108.9 %shard_map.95 = (bf16[5,20,1024]{2,1,0:T(8,128)(2,1)}, bf16[5,20,1024]{2,1,0:T(8,128)(2,1)}) custom-call(s32[1,32]{1,0:T(1,128)} %bitcast.5, s32[2,32]{1,0:T(2,128)} %bitcast.4, s32[32]{0:T(128)} %valid_ref.1, f32[5,20]{1,0:T(8,128)} %rate_ref.1, s32[8,128]{1,0:T(8,128)} %bitcast.3, bf16[5,20,1024]{2,1,0:T(8,128)(2,1)} %ice_hbm.1, ...), custom_call_target="tpu_custom_call" | custom-call | tf_op jit(solution)/shard_map/pallas_call | solution.py:535
  109.6 0.0 copy-start
  109.6 1.7 %copy.12 = bf16[5,20,1024]{2,1,0:T(8,128)(2,1)} copy(bf16[5,20,1024]{2,1,0:T(8,128)(2,1)} %get-tuple-element.4) | data formatting | bytes 409600
  111.3 0.0 copy-done
  111.3 0.7 copy.13
Async XLA Ops:
  109.6 1.7 %copy-start = (bf16[5,20,1024]{2,1,0:T(8,128)(2,1)S(1)}, bf16[5,20,1024]{2,1,0:T(8,128)(2,1)}, u32[]{:S(2)}) copy-start(bf16[5,20,1024]{2,1,0:T(8,128)(2,1)} %get-tuple-element.5) | copy-start | bytes 614404

commit v2 on v1

--- a/solution.py
+++ b/solution.py
@@ -18,7 +18,7 @@
 def order(count, calls):
     steps = []
     for h in range(count):
-        for place, call in zip((0, 1, 5, 7, 12, 16, 22), calls):
+        for place, call in zip((0, 1, 4, 7, 12, 16, 22), calls):
             steps.append((3 * h + place, h, call))
     return [step[1:] for step in sorted(steps, key=lambda step: step[:2])]
 
@@ -84,7 +84,7 @@
     pl.semaphore_signal(barrier, inc=1, device_id=partner, device_id_type=pl.DeviceIdType.MESH)
 
     def acopy(h, j):
-        return remote(ice_g[h].at[0], ice_g[h].at[j], as_s.at[h, j], as_r.at[h, j], chip(j))
+        return remote(ice_g[h].at[0], ice_g[h].at[j], as_s.at[h], as_r.at[h], chip(j))
 
     def ncopy(j):
         return remote(namv.at[j], namv.at[Q + j], ns_s.at[j], ns_r.at[j], chip(j))
@@ -94,10 +94,31 @@
 
     def pcopy(h, g, j):
         at = pl.ds(zord[g] * per, per)
-        return remote(psend[h].at[j, at], prec[h].at[j, at], ps_s.at[h, g, j], ps_r.at[h, g, j], chip(j))
+        return remote(psend[h].at[j, at], prec[h].at[j, at], ps_s.at[h, g], ps_r.at[h, g], chip(j))
+
+    others = pl.ds(1, Q - 1)
+
+    def every(src, dst, s, r):
+        return remote(src, dst, s, r, partner)
+
+    def pall(h, g):
+        at = pl.ds(zord[g] * per, per)
+        return every(psend[h].at[others, at], prec[h].at[others, at], ps_s.at[h, g], ps_r.at[h, g])
+
+    def aall(h):
+        return every(ice_g[h].at[others], ice_g[h].at[others], as_s.at[h], as_r.at[h])
+
+    def call(h):
+        return every(csend[h].at[others], crec[h].at[others], cs_s.at[h], cs_r.at[h])
+
+    def gall(h):
+        return every(fb[h].at[c], fb[h].at[1 - c], gs_s.at[h], gs_r.at[h])
+
+    def dall(h):
+        return every(dsend[h], drec[h], ds_s.at[h], ds_s.at[h])
 
     def dcopy(h, zd):
-        return remote(dsend[h].at[zd], drec[h].at[zd], ds_s.at[h, zd], ds_r.at[h, zd], partner)
+        return remote(dsend[h].at[zd], drec[h].at[zd], ds_s.at[h], ds_r.at[h, zd], partner)
 
     def zcopy(h, zd):
         return remote(zsend[h].at[zd], zrec[h].at[z], zs_s.at[h, zd], zs_r.at[h, z], line(zd))
@@ -119,14 +140,10 @@
         return remote(held, held, fr_s.at[h, g], fs_r.at[h, zord[g]], line(zord[2]))
 
     def gcopy(h, zs):
-        return remote(fb[h].at[c, zs], fb[h].at[c, zs], gs_s.at[h, zs], gs_r.at[h, zs], partner)
-
-    def gwait(h, zs):
-        held = fb[h].at[1 - c, zs]
-        remote(held, held, gs_s.at[h, zs], gs_r.at[h, zs], partner).wait_recv()
+        return remote(fb[h].at[c, zs], fb[h].at[c, zs], gs_s.at[h], gs_r.at[h], partner)
 
     def ccopy(h, j):
-        return remote(csend[h].at[j], crec[h].at[j], cs_s.at[h, j], cs_r.at[h, j], chip(j, True))
+        return remote(csend[h].at[j], crec[h].at[j], cs_s.at[h], cs_r.at[h], chip(j, True))
 
     def lanes(t):
         return pl.ds(t * LANES, LANES)
@@ -346,8 +363,7 @@
         return accs
 
     def fluxes(h):
-        for zs in range(Z):
-            gwait(h, zs)
+        gall(h).wait_recv()
 
     def give(h, j):
         accs = back(h, j)
@@ -372,11 +388,9 @@
 
     def finish(h, number):
         first, count = parts[h]
-        for j in range(Q - 1, 0, -1):
-            ccopy(h, j).wait_recv()
+        call(h).wait_recv()
         if number:
-            for j in range(1, Q):
-                acopy(h, j).wait_send()
+            aall(h).wait_send()
         rate = rates[pl.ds(first, count), :]
         for t in range(tiles):
             acc = mine[h][t]
@@ -392,11 +406,9 @@
             for j in range(Q - 1, 0, -1):
                 acopy(h, j).start()
 
-        for j in range(1, Q):
-            ccopy(h, j).wait_send()
-        for zd in range(Z):
-            dcopy(h, zd).wait_send()
-            gcopy(h, zd).wait_send()
+        call(h).wait_send()
+        dall(h).wait_send()
+        gall(h).wait_send()
         zcopy(h, zord[2]).wait_send()
         for g in (1, 2):
             fcopy(h, zord[g]).wait_send()
@@ -413,8 +425,7 @@
                 frelay(h, g).wait_send()
 
     def arrive(h):
-        for j in range(Q - 1, 0, -1):
-            acopy(h, j).wait_recv()
+        aall(h).wait_recv()
 
     def again(h):
         arrive(h)
@@ -431,8 +442,7 @@
 
     for g in range(Z):
         for h in range(H):
-            for j in range(Q - 1, 0, -1):
-                pcopy(h, g, j).wait_recv()
+            pall(h, g).wait_recv()
             forward(h, zord[g], True)
         for h in range(H):
             merge(h, g)
@@ -473,9 +483,9 @@
     for j in range(1, Q):
         wcopy(j).wait_send()
         ncopy(j).wait_send()
-        for h in range(H):
-            for g in range(Z):
-                pcopy(h, g, j).wait_send()
+    for h in range(H):
+        for g in range(Z):
+            pall(h, g).wait_send()
 
     def send(r, held, out):
         for t in range(tiles):
@@ -491,9 +501,9 @@
             if first < (r + 1) * fields <= first + count:
                 send(r, res, ice_out)
 
-    for h, call in order(H, (again, merges, relay, flux, arrivals, backward, last)):
-        if h or call not in (again, merges):
-            call(h)
+    for h, step in order(H, (again, merges, relay, flux, arrivals, backward, last)):
+        if h or step not in (again, merges):
+            step(h)
 
 
 def cut(chans):
@@ -566,15 +576,15 @@
             pltpu.SemaphoreType.DMA,
             sems(Q), sems(Q), sems(Q),
             sems(Q), sems(Q),
-            sems(H, Z, Q), sems(H, Z, Q),
-            sems(H, Q), sems(H, Q),
             sems(H, Z), sems(H, Z),
+            sems(H), sems(H),
+            sems(H), sems(H, Z),
             sems(H, Z), sems(H, Z),
             sems(H, 2), sems(H, 2),
             sems(H, Z), sems(H, Z),
             sems(H, 2),
-            sems(H, Z), sems(H, Z),
-            sems(H, Q), sems(H, Q),
+            sems(H), sems(H),
+            sems(H), sems(H),
             pltpu.VMEM((tiles, width), jnp.int32),
             pltpu.VMEM(ice_state.shape, jnp.bfloat16),
             pltpu.VMEM(ice_state.shape, jnp.bfloat16),

time: 112 us -> 109 us (0.973)
  Pallas kernels: 109 us -> 106 us
    pallas_call x1, Pallas kernels: 109 us -> 106 us  [on_device(): pl.pallas_call(functools.partial(kernel, (X, Y, Z, tiles, blocks), parts)...]
where the time goes in v2:
time: 109 us
  Pallas kernels  106 us (97%)
  local copies, waits for them, and re-layouts  2.39 us (2%)
    pallas_call x1, Pallas kernels, on_device(): pl.pallas_call(functools.partial(kernel, (X, Y, Z, tiles, blocks), parts)...  106 us
    unnamed x4, local copies, waits for them, and re-layouts  2.39 us

profile of v2, /device:TPU:0, one launch (start us, length us, event | category | flops | bytes accessed | tf_op | source)
XLA Modules:
  0.0 108.9 jit_solution(6550142758419422868)
XLA Ops:
  0.6 105.9 %shard_map.95 = (bf16[5,20,1024]{2,1,0:T(8,128)(2,1)}, bf16[5,20,1024]{2,1,0:T(8,128)(2,1)}) custom-call(s32[1,32]{1,0:T(1,128)} %bitcast.5, s32[2,32]{1,0:T(2,128)} %bitcast.4, s32[32]{0:T(128)} %valid_ref.1, f32[5,20]{1,0:T(8,128)} %rate_ref.1, s32[8,128]{1,0:T(8,128)} %bitcast.3, bf16[5,20,1024]{2,1,0:T(8,128)(2,1)} %ice_hbm.1, ...), custom_call_target="tpu_custom_call" | custom-call | tf_op jit(solution)/shard_map/pallas_call | solution.py:545
  106.5 0.0 copy-start
  106.6 1.7 %copy.12 = bf16[5,20,1024]{2,1,0:T(8,128)(2,1)} copy(bf16[5,20,1024]{2,1,0:T(8,128)(2,1)} %get-tuple-element.4) | data formatting | bytes 409600
  108.3 0.0 copy-done
  108.3 0.7 copy.13
Async XLA Ops:
  106.5 1.7 %copy-start = (bf16[5,20,1024]{2,1,0:T(8,128)(2,1)S(1)}, bf16[5,20,1024]{2,1,0:T(8,128)(2,1)}, u32[]{:S(2)}) copy-start(bf16[5,20,1024]{2,1,0:T(8,128)(2,1)} %get-tuple-element.5) | copy-start | bytes 614404
